TPU v7x, 32 devices: a whole 2x2x4 slice. The times are simulated.
32 devices in a mesh: grp: 16 (over z, y, core), seq: 2 (over x).
Axes of the slice: x: 2, y: 2, z: 4, core: 2. Of those that a mesh axis runs over, the one named last changes fastest.
Arguments:
- queries: bfloat16 [8192, 4096], P(('grp', 'seq')), may hold values from -8 to 8
- keys: bfloat16 [8192, 4096], P(('grp', 'seq')), may hold values from -6 to 6
- values: bfloat16 [8192, 4096], P(('grp', 'seq')), may hold values from -6 to 6
- global_pos: int32 [64], P(('grp', 'seq')), may hold values from 0 to 127
- layout: int32 [64, 32], P(('grp', 'seq')), may hold values from 0 to 63, all different within a row
Outputs:
- attended: bfloat16 [8192, 4096], P(('grp', 'seq'))
Inputs may be any that keep to these rules, and one draw needn't show every extreme that they name: `layout`: each row lists 32 different block indices, and every block is listed by some row.
All inputs are finite; a program needn't handle non-finite values.
Results may differ from a plain program's by a relative error of at most 0.0042.
Values may be sent and summed in bfloat16 or wider, within the bound.
A program may use at most 128 MiB of HBM per device.

v0:
```python
import functools
import math

import jax
import jax.numpy as jnp
from jax import lax
from jax.experimental import pallas as pl
from jax.experimental.pallas import tpu as pltpu
from jax.sharding import PartitionSpec as P

HEAD_DIM = 128
BLOCK = 128
CHUNK_HEADS = 2
EARLY_CHUNKS = 4
POOL_HEADS = 8
MESH = pl.DeviceIdType.MESH


def dot_t(a, b):
    return lax.dot_general(a, b, (((1,), (1,)), ((), ())), preferred_element_type=jnp.float32)


def dot(a, b):
    return jnp.dot(a, b, preferred_element_type=jnp.float32)


def kernel(
    groups, seqs, pos_hbm, layout_hbm, q_hbm, k_hbm, v_hbm, out,
    pos_ref, layout_ref, q, k, v, halo, gathered, own, wide, bias,
    load_sem, send_sem, recv_sem, seq_send, seq_recv, grp_send, grp_recv,
):
    rows, width = q.shape
    heads = width // HEAD_DIM
    blocks = rows // BLOCK
    devices = groups * seqs
    total_blocks = devices * blocks
    step_cols = CHUNK_HEADS * HEAD_DIM
    chunks = heads // CHUNK_HEADS
    stages = groups.bit_length() - 1
    near = 2 * seqs

    g, s = lax.axis_index("grp"), lax.axis_index("seq")
    me = g * seqs + s
    has_left, has_right = me > 0, me < devices - 1
    left, right = lax.max(me - 1, 0), lax.min(me + 1, devices - 1)

    def coords(position):
        return (position // seqs, position % seqs)

    left_near = has_left & (me % near != 0)
    right_near = has_right & ((me + 1) % near != 0)
    left_far = has_left & (me % near == 0)
    right_far = has_right & ((me + 1) % near == 0)

    loads = [
        pltpu.make_async_copy(src, dst, load_sem.at[i])
        for i, (src, dst) in enumerate(((k_hbm, k), (v_hbm, v), (q_hbm, q), (pos_hbm, pos_ref), (layout_hbm, layout_ref)))
    ]
    barrier = pltpu.get_barrier_semaphore()

    def signal(device):
        pl.semaphore_signal(barrier, inc=1, device_id=device, device_id_type=MESH)

    @pl.when(has_left)
    def _():
        signal(coords(left))

    @pl.when(has_right)
    def _():
        signal(coords(right))

    for o in range(1, seqs):
        signal((g, lax.rem(s + o, seqs)))

    def partner(stage):
        size = 1 << stage
        bit = (g // size) % 2
        return g + size * (1 - 2 * bit)

    for stage in range(stages):
        signal((partner(stage), s))
    for load in loads:
        load.start()
    pl.semaphore_wait(
        barrier, seqs - 1 + stages + has_left.astype(jnp.int32) + has_right.astype(jnp.int32)
    )

    def edge(side, kv, c):
        src = (k, v)[kv]
        cols = pl.ds(pl.multiple_of(c * step_cols, step_cols), step_cols)
        first = rows - BLOCK if side == 0 else 0
        return pltpu.make_async_remote_copy(
            src_ref=src.at[pl.ds(first, BLOCK), cols],
            dst_ref=halo.at[side, kv, :, cols],
            send_sem=send_sem.at[side, kv, c],
            recv_sem=recv_sem.at[side, kv, c],
            device_id=coords(right if side == 0 else left),
            device_id_type=MESH,
        )

    def send_edges(side, when, lo, hi):
        @pl.when(when)
        def _():
            def body(c, carry):
                for kv in range(2):
                    edge(side, kv, c).start()
                return carry

            lax.fori_loop(lo, hi, body, 0)

    def send_both(when_right, when_left, lo, hi):
        both = when_right & when_left

        @pl.when(both)
        def _():
            def body(c, carry):
                for side in range(2):
                    for kv in range(2):
                        edge(side, kv, c).start()
                return carry

            lax.fori_loop(lo, hi, body, 0)

        send_edges(0, when_right & jnp.logical_not(when_left), lo, hi)
        send_edges(1, when_left & jnp.logical_not(when_right), lo, hi)

    loads[0].wait()
    loads[1].wait()
    early = min(EARLY_CHUNKS, chunks)
    later = (early + chunks) // 2
    send_both(right_near, left_near, 0, early)

    picks = (
        lax.broadcasted_iota(jnp.int32, (16, rows), 1) // BLOCK
        == lax.broadcasted_iota(jnp.int32, (16, rows), 0)
    ).astype(jnp.bfloat16)

    def pool(step, carry):
        for i in range(POOL_HEADS):
            h = step * POOL_HEADS + i
            cols = pl.ds(pl.multiple_of(h * HEAD_DIM, HEAD_DIM), HEAD_DIM)
            for kv, src in enumerate((k, v)):
                mean = dot(picks, src[:, cols])[:8] * (1.0 / BLOCK)
                spread = jnp.mean(mean * mean, axis=-1, keepdims=True)
                scaled = mean / jnp.sqrt(spread + 1e-06)
                for b in range(blocks):
                    own[pl.ds((kv * blocks + b) * heads + h, 1), :] = scaled[b : b + 1]
        return carry

    lax.fori_loop(0, heads // POOL_HEADS, pool, 0)
    gathered[me] = own[...].astype(jnp.bfloat16)

    def seq_copy(o):
        return pltpu.make_async_remote_copy(
            src_ref=gathered.at[pl.ds(me, 1)],
            dst_ref=gathered.at[pl.ds(me, 1)],
            send_sem=seq_send.at[o],
            recv_sem=seq_recv.at[o],
            device_id=(g, lax.rem(s + o, seqs)),
            device_id_type=MESH,
        )

    for o in range(1, seqs):
        seq_copy(o).start()

    send_both(right_near, left_near, early, chunks)

    loads[3].wait()
    loads[4].wait()
    ids = lax.broadcasted_iota(jnp.int32, (BLOCK, total_blocks), 1)
    spots = lax.broadcasted_iota(jnp.int32, (BLOCK, total_blocks), 0)
    for b in range(blocks):
        seen = spots == pos_ref[b]
        for link in range(layout_ref.shape[1]):
            seen = seen | (ids == layout_ref[b, link])
        bias[b * BLOCK : (b + 1) * BLOCK, :] = jnp.where(seen, 0.0, -jnp.inf)

    @pl.when(jnp.logical_not(has_left))
    def _():
        halo[0] = jnp.zeros(halo.shape[1:], halo.dtype)

    @pl.when(jnp.logical_not(has_right))
    def _():
        halo[1] = jnp.zeros(halo.shape[1:], halo.dtype)

    for o in range(1, seqs):
        seq_copy(o).wait()

    def grp_copy(stage):
        size = (1 << stage) * seqs
        first = (g // (1 << stage)) * size
        return pltpu.make_async_remote_copy(
            src_ref=gathered.at[pl.ds(first, size)],
            dst_ref=gathered.at[pl.ds(first, size)],
            send_sem=grp_send.at[stage],
            recv_sem=grp_recv.at[stage],
            device_id=(partner(stage), s),
            device_id_type=MESH,
        )

    for stage in range(stages):
        grp_copy(stage).start()
        if stage == stages - 2:
            send_both(right_far, left_far, 0, later)
        if stage == stages - 1:
            send_both(right_far, left_far, later if stages > 1 else early, chunks)
        grp_copy(stage).wait()

    def widen(d, carry):
        spread = blocks * heads
        at = pl.ds(pl.multiple_of(d * spread, spread), spread)
        for kv in range(2):
            wide[kv, at, :] = gathered[d, kv * spread : (kv + 1) * spread].astype(jnp.float32)
        return carry

    lax.fori_loop(0, devices, widen, 0)
    loads[2].wait()

    factor = math.log2(math.e) / math.sqrt(HEAD_DIM)
    left_bias = jnp.where(has_left, 0.0, -jnp.inf)
    right_bias = jnp.where(has_right, 0.0, -jnp.inf)

    def attend(c, carry):
        for side, there in ((0, has_left), (1, has_right)):
            @pl.when(there)
            def _(side=side):
                for kv in range(2):
                    edge(side, kv, c).wait_recv()

        for i in range(CHUNK_HEADS):
            h = c * CHUNK_HEADS + i
            cols = pl.ds(pl.multiple_of(h * HEAD_DIM, HEAD_DIM), HEAD_DIM)
            rows_of = pl.ds(h, total_blocks, stride=heads)
            qh, kh, vh = q[:, cols], k[:, cols], v[:, cols]
            sk = wide[0, rows_of, :].astype(jnp.bfloat16)
            sv = wide[1, rows_of, :].astype(jnp.bfloat16)
            kl, vl = halo[0, 0, :, cols], halo[0, 1, :, cols]
            kr, vr = halo[1, 0, :, cols], halo[1, 1, :, cols]
            s_own = dot_t(qh, kh)
            if blocks > 2:
                gap = (
                    lax.broadcasted_iota(jnp.int32, (rows, rows), 0) // BLOCK
                    - lax.broadcasted_iota(jnp.int32, (rows, rows), 1) // BLOCK
                )
                s_own = jnp.where(jnp.abs(gap) <= 1, s_own, -jnp.inf)
            s_left = dot_t(qh[:BLOCK], kl) + left_bias
            s_right = dot_t(qh[rows - BLOCK :], kr) + right_bias
            s_sum = dot_t(qh, sk) + bias[...]
            middle = [jnp.full((rows - 2 * BLOCK, BLOCK), -jnp.inf)] if blocks > 2 else []
            s_halo = jnp.concatenate([s_left, *middle, s_right], axis=0)
            peak = jnp.maximum(
                jnp.max(s_sum, axis=-1, keepdims=True),
                jnp.maximum(
                    jnp.max(s_own, axis=-1, keepdims=True),
                    jnp.max(s_halo, axis=-1, keepdims=True),
                ),
            )
            w_own = jnp.exp2((s_own - peak) * factor)
            w_halo = jnp.exp2((s_halo - peak) * factor)
            w_sum = jnp.exp2((s_sum - peak) * factor)
            total = (
                jnp.sum(w_own, axis=-1, keepdims=True)
                + jnp.sum(w_halo, axis=-1, keepdims=True)
                + jnp.sum(w_sum, axis=-1, keepdims=True)
            )
            r_halo = w_halo.astype(jnp.bfloat16)
            acc = dot(w_own.astype(jnp.bfloat16), vh) + dot(w_sum.astype(jnp.bfloat16), sv)
            middle = [jnp.zeros((rows - 2 * BLOCK, HEAD_DIM), jnp.float32)] if blocks > 2 else []
            acc = acc + jnp.concatenate(
                [dot(r_halo[:BLOCK], vl), *middle, dot(r_halo[rows - BLOCK :], vr)], axis=0
            )
            out[:, cols] = (acc / total).astype(jnp.bfloat16)
        return carry

    lax.fori_loop(0, chunks, attend, 0)

    def finish(c, carry):
        for side, there in ((0, has_right), (1, has_left)):
            @pl.when(there)
            def _(side=side):
                for kv in range(2):
                    edge(side, kv, c).wait_send()
        return carry

    lax.fori_loop(0, chunks, finish, 0)


def solution(mesh):
    groups, seqs = mesh.shape["grp"], mesh.shape["seq"]
    assert groups & (groups - 1) == 0

    def shards(queries, keys, values, global_pos, layout):
        rows, width = queries.shape
        blocks, heads = rows // BLOCK, width // HEAD_DIM
        devices = groups * seqs
        chunks = heads // CHUNK_HEADS
        stages = groups.bit_length() - 1
        summaries = devices * blocks * width
        limit = 2 * (4 * rows + 4 * BLOCK) * width + 12 * summaries + (8 << 20)
        operands = [
            pltpu.with_memory_space_constraint(a, pltpu.HBM)
            for a in (global_pos, layout, queries, keys, values)
        ]
        return pl.pallas_call(
            functools.partial(kernel, groups, seqs),
            out_shape=pltpu.VMEM((rows, width), jnp.bfloat16),
            in_specs=[pl.BlockSpec(memory_space=pltpu.HBM)] * 5,
            out_specs=pl.BlockSpec(memory_space=pltpu.VMEM),
            scratch_shapes=[
                pltpu.SMEM(global_pos.shape, jnp.int32),
                pltpu.SMEM(layout.shape, jnp.int32),
                pltpu.VMEM((rows, width), jnp.bfloat16),
                pltpu.VMEM((rows, width), jnp.bfloat16),
                pltpu.VMEM((rows, width), jnp.bfloat16),
                pltpu.VMEM((2, 2, BLOCK, width), jnp.bfloat16),
                pltpu.VMEM((devices, 2 * blocks * heads, HEAD_DIM), jnp.bfloat16),
                pltpu.VMEM((2 * blocks * heads, HEAD_DIM), jnp.float32),
                pltpu.VMEM((2, devices * blocks * heads, HEAD_DIM), jnp.float32),
                pltpu.VMEM((rows, devices * blocks), jnp.float32),
                pltpu.SemaphoreType.DMA((5,)),
                pltpu.SemaphoreType.DMA((2, 2, chunks)),
                pltpu.SemaphoreType.DMA((2, 2, chunks)),
                pltpu.SemaphoreType.DMA((seqs,)),
                pltpu.SemaphoreType.DMA((seqs,)),
                pltpu.SemaphoreType.DMA((max(stages, 1),)),
                pltpu.SemaphoreType.DMA((max(stages, 1),)),
            ],
            compiler_params=pltpu.CompilerParams(
                collective_id=0, has_side_effects=True, vmem_limit_bytes=limit
            ),
        )(*operands)

    both = ("grp", "seq")
    in_specs = (P(both, None), P(both, None), P(both, None), P(both), P(both, None))
    return jax.shard_map(
        shards, mesh=mesh, in_specs=in_specs, out_specs=P(both, None), check_vma=False
    )
```

profile of v0, /device:TPU:0, one launch (start us, length us, event | category | flops | bytes accessed | tf_op | source)
XLA Modules:
  0.0 100.4 jit_solution(11832801148701795260)
XLA Ops:
  0.0 99.0 %shard_map.55 = bf16[256,4096]{1,0:T(8,128)(2,1)S(1)} custom-call(s32[2]{0:T(128)} %pos_hbm.1, s32[2,32]{1,0:T(2,128)} %layout_hbm.1, bf16[256,4096]{1,0:T(8,128)(2,1)} %q_hbm.1, bf16[256,4096]{1,0:T(8,128)(2,1)} %k_hbm.1, bf16[256,4096]{1,0:T(8,128)(2,1)} %v_hbm.1), custom_call_target="tpu_custom_call" | custom-call | tf_op jit(solution)/shard_map/pallas_call | solution.py:304
  99.1 1.3 %copy.7 = bf16[256,4096]{1,0:T(8,128)(2,1)} copy(bf16[256,4096]{1,0:T(8,128)(2,1)S(1)} %shard_map.55) | data formatting | bytes 4194304
where the time goes:
time: 101 us; the launch traced here: 100 us
  Pallas kernels  99 us (98%)
  local copies, waits for them, and re-layouts  1.32 us (1%)
    pallas_call x1, Pallas kernels, shards(): pl.pallas_call(functools.partial(kernel, groups, seqs), out_shape=pltpu.V...  99 us

commit v1 on v0

--- a/solution.py
+++ b/solution.py
@@ -11,7 +11,8 @@
 HEAD_DIM = 128
 BLOCK = 128
 CHUNK_HEADS = 2
-EARLY_CHUNKS = 4
+EARLY_CHUNKS = 2
+PLANE_BITS = 2
 POOL_HEADS = 8
 MESH = pl.DeviceIdType.MESH
 
@@ -26,8 +27,9 @@
 
 def kernel(
     groups, seqs, pos_hbm, layout_hbm, q_hbm, k_hbm, v_hbm, out,
-    pos_ref, layout_ref, q, k, v, halo, gathered, own, wide, bias,
-    load_sem, send_sem, recv_sem, seq_send, seq_recv, grp_send, grp_recv,
+    pos_ref, layout_ref, q, k, v, halo, relay, gathered, own, wide, bias,
+    load_sem, send_sem, recv_sem, relay_recv, relay_send, seq_send, seq_recv,
+    line_send, line_recv, bit_send, bit_recv,
 ):
     rows, width = q.shape
     heads = width // HEAD_DIM
@@ -36,21 +38,39 @@
     total_blocks = devices * blocks
     step_cols = CHUNK_HEADS * HEAD_DIM
     chunks = heads // CHUNK_HEADS
-    stages = groups.bit_length() - 1
-    near = 2 * seqs
+    bits, planes = gather_shape(groups)
+    low = 1 << bits
+    relaying = relays(groups, seqs)
 
     g, s = lax.axis_index("grp"), lax.axis_index("seq")
     me = g * seqs + s
     has_left, has_right = me > 0, me < devices - 1
-    left, right = lax.max(me - 1, 0), lax.min(me + 1, devices - 1)
+    plane, lane = g // low, g % low
 
     def coords(position):
         return (position // seqs, position % seqs)
 
-    left_near = has_left & (me % near != 0)
-    right_near = has_right & ((me + 1) % near != 0)
-    left_far = has_left & (me % near == 0)
-    right_far = has_right & ((me + 1) % near == 0)
+    first = s % 2
+    second = 1 - first
+
+    def exists(side):
+        return jnp.where(side == 0, has_right, has_left)
+
+    def neighbour(side):
+        return jnp.clip(me + 1 - 2 * side, 0, devices - 1)
+
+    pairs = groups // 2
+    step_pair = 2 * seqs
+    far = (g % 2 == s) if relaying else False
+    rank = jnp.where(s == 0, g // 2, pairs - 1 - g // 2)
+    odd = rank % 2 == 1
+    across = me + (step_pair - 1) * (1 - 2 * s)
+    behind, ahead = me + step_pair * (1 - 2 * s), me - step_pair * (1 - 2 * s)
+    handed = jnp.where(far, chunks * jnp.where(odd, 1, rank) // pairs, 0) if relaying else 0
+    via = jnp.where(odd, ahead, across)
+    passing = chunks * jnp.where(odd, pairs - 1 - rank, 1) // pairs
+    target = jnp.where(odd, behind, across)
+    target_side = jnp.where(odd, first, second)
 
     loads = [
         pltpu.make_async_copy(src, dst, load_sem.at[i])
@@ -58,78 +78,115 @@
     ]
     barrier = pltpu.get_barrier_semaphore()
 
-    def signal(device):
-        pl.semaphore_signal(barrier, inc=1, device_id=device, device_id_type=MESH)
-
-    @pl.when(has_left)
-    def _():
-        signal(coords(left))
-
-    @pl.when(has_right)
-    def _():
-        signal(coords(right))
-
-    for o in range(1, seqs):
-        signal((g, lax.rem(s + o, seqs)))
-
-    def partner(stage):
-        size = 1 << stage
-        bit = (g // size) % 2
-        return g + size * (1 - 2 * bit)
-
-    for stage in range(stages):
-        signal((partner(stage), s))
+    peers = [(exists(side), neighbour(side)) for side in range(2)]
+    peers += [(True, g * seqs + lax.rem(s + o, seqs)) for o in range(1, seqs)]
+    peers += [(True, (g ^ (1 << bit)) * seqs + s) for bit in range(bits)]
+    if planes > 1:
+        peers += [
+            (plane > 0, jnp.maximum(me - low * seqs, 0)),
+            (plane < planes - 1, jnp.minimum(me + low * seqs, devices - 1)),
+        ]
+    if relaying:
+        peers += [(far, across), (far & (rank > 0), ahead), (far & (rank < pairs - 1), behind)]
     for load in loads:
         load.start()
-    pl.semaphore_wait(
-        barrier, seqs - 1 + stages + has_left.astype(jnp.int32) + has_right.astype(jnp.int32)
-    )
+    expected = 0
+    for there, peer in peers:
+        if there is True:
+            pl.semaphore_signal(barrier, inc=1, device_id=coords(peer), device_id_type=MESH)
+            expected = expected + 1
+        else:
+            @pl.when(there)
+            def _(peer=peer):
+                pl.semaphore_signal(barrier, inc=1, device_id=coords(peer), device_id_type=MESH)
+            expected = expected + there.astype(jnp.int32)
+    pl.semaphore_wait(barrier, expected)
+
+    def columns(c):
+        return pl.ds(pl.multiple_of(c * step_cols, step_cols), step_cols)
 
     def edge(side, kv, c):
-        src = (k, v)[kv]
-        cols = pl.ds(pl.multiple_of(c * step_cols, step_cols), step_cols)
-        first = rows - BLOCK if side == 0 else 0
-        return pltpu.make_async_remote_copy(
-            src_ref=src.at[pl.ds(first, BLOCK), cols],
-            dst_ref=halo.at[side, kv, :, cols],
+        start = pl.multiple_of((rows - BLOCK) * (1 - side), BLOCK)
+        return pltpu.make_async_remote_copy(
+            src_ref=(k_hbm, v_hbm)[kv].at[pl.ds(start, BLOCK), columns(c)],
+            dst_ref=halo.at[side, kv, :, columns(c)],
             send_sem=send_sem.at[side, kv, c],
             recv_sem=recv_sem.at[side, kv, c],
-            device_id=coords(right if side == 0 else left),
-            device_id_type=MESH,
-        )
-
-    def send_edges(side, when, lo, hi):
-        @pl.when(when)
-        def _():
-            def body(c, carry):
-                for kv in range(2):
-                    edge(side, kv, c).start()
-                return carry
-
-            lax.fori_loop(lo, hi, body, 0)
-
-    def send_both(when_right, when_left, lo, hi):
-        both = when_right & when_left
+            device_id=coords(neighbour(side)),
+            device_id_type=MESH,
+        )
+
+    def hand(kv, c):
+        start = pl.multiple_of((rows - BLOCK) * (1 - second), BLOCK)
+        return pltpu.make_async_remote_copy(
+            src_ref=(k_hbm, v_hbm)[kv].at[pl.ds(start, BLOCK), columns(c)],
+            dst_ref=relay.at[kv, :, columns(c)],
+            send_sem=send_sem.at[second, kv, c],
+            recv_sem=relay_recv.at[kv, c],
+            device_id=coords(jnp.clip(via, 0, devices - 1)),
+            device_id_type=MESH,
+        )
+
+    def forward(kv, c):
+        return pltpu.make_async_remote_copy(
+            src_ref=relay.at[kv, :, columns(c)],
+            dst_ref=halo.at[target_side, kv, :, columns(c)],
+            send_sem=relay_send.at[kv, c],
+            recv_sem=recv_sem.at[target_side, kv, c],
+            device_id=coords(jnp.clip(target, 0, devices - 1)),
+            device_id_type=MESH,
+        )
+
+    def pass_on(kv, c):
+        hand(kv, c).wait_recv()
+        forward(kv, c).start()
+
+    def each(lo, hi, act):
+        def body(c, carry):
+            for kv in range(2):
+                act(kv, c)
+            return carry
+
+        lax.fori_loop(lo, hi, body, 0)
+
+    early = min(EARLY_CHUNKS, chunks)
+
+    def send(lo, hi):
+        both = exists(first) & exists(second)
+
+        def pair(kv, c):
+            edge(first, kv, c).start()
+
+            if not relaying:
+                edge(second, kv, c).start()
+                return
+
+            @pl.when(c < handed)
+            def _():
+                hand(kv, c).start()
+
+            @pl.when(c >= handed)
+            def _():
+                edge(second, kv, c).start()
 
         @pl.when(both)
         def _():
-            def body(c, carry):
-                for side in range(2):
-                    for kv in range(2):
-                        edge(side, kv, c).start()
-                return carry
-
-            lax.fori_loop(lo, hi, body, 0)
-
-        send_edges(0, when_right & jnp.logical_not(when_left), lo, hi)
-        send_edges(1, when_left & jnp.logical_not(when_right), lo, hi)
+            each(lo, hi, pair)
+
+        @pl.when(exists(first) & jnp.logical_not(both))
+        def _():
+            each(lo, hi, lambda kv, c: edge(first, kv, c).start())
+
+    @pl.when(me != 1)
+    def _():
+        send(0, early)
+
+    @pl.when(me == 1)
+    def _():
+        each(0, early, lambda kv, c: edge(first, kv, c).start())
 
     loads[0].wait()
     loads[1].wait()
-    early = min(EARLY_CHUNKS, chunks)
-    later = (early + chunks) // 2
-    send_both(right_near, left_near, 0, early)
-
     picks = (
         lax.broadcasted_iota(jnp.int32, (16, rows), 1) // BLOCK
         == lax.broadcasted_iota(jnp.int32, (16, rows), 0)
@@ -148,12 +205,14 @@
         return carry
 
     lax.fori_loop(0, heads // POOL_HEADS, pool, 0)
-    gathered[me] = own[...].astype(jnp.bfloat16)
+    digits = [(lane >> bit) % 2 for bit in reversed(range(bits))]
+    gathered[(plane, *digits, s)] = own[...].astype(jnp.bfloat16)
 
     def seq_copy(o):
-        return pltpu.make_async_remote_copy(
-            src_ref=gathered.at[pl.ds(me, 1)],
-            dst_ref=gathered.at[pl.ds(me, 1)],
+        mine = gathered.at[(pl.ds(plane, 1), *(pl.ds(d, 1) for d in digits), pl.ds(s, 1))]
+        return pltpu.make_async_remote_copy(
+            src_ref=mine,
+            dst_ref=mine,
             send_sem=seq_send.at[o],
             recv_sem=seq_recv.at[o],
             device_id=(g, lax.rem(s + o, seqs)),
@@ -163,7 +222,19 @@
     for o in range(1, seqs):
         seq_copy(o).start()
 
-    send_both(right_near, left_near, early, chunks)
+    if relaying:
+        @pl.when(far & jnp.logical_not(odd))
+        def _():
+            each(0, passing, pass_on)
+
+    @pl.when(me != 1)
+    def _():
+        send(early, chunks)
+
+    @pl.when(me == 1)
+    def _():
+        each(early, chunks, lambda kv, c: edge(first, kv, c).start())
+        each(0, chunks, lambda kv, c: edge(second, kv, c).start())
 
     loads[3].wait()
     loads[4].wait()
@@ -186,31 +257,61 @@
     for o in range(1, seqs):
         seq_copy(o).wait()
 
-    def grp_copy(stage):
-        size = (1 << stage) * seqs
-        first = (g // (1 << stage)) * size
-        return pltpu.make_async_remote_copy(
-            src_ref=gathered.at[pl.ds(first, size)],
-            dst_ref=gathered.at[pl.ds(first, size)],
-            send_sem=grp_send.at[stage],
-            recv_sem=grp_recv.at[stage],
-            device_id=(partner(stage), s),
-            device_id_type=MESH,
-        )
-
-    for stage in range(stages):
-        grp_copy(stage).start()
-        if stage == stages - 2:
-            send_both(right_far, left_far, 0, later)
-        if stage == stages - 1:
-            send_both(right_far, left_far, later if stages > 1 else early, chunks)
-        grp_copy(stage).wait()
+    def line_copy(way, step):
+        there = jnp.clip(plane + 1 - 2 * way, 0, planes - 1)
+        part = jnp.clip(plane + (step - 1) * (2 * way - 1), 0, planes - 1)
+        part = gathered.at[(pl.ds(part, 1), *(pl.ds(d, 1) for d in digits))]
+        return pltpu.make_async_remote_copy(
+            src_ref=part,
+            dst_ref=part,
+            send_sem=line_send.at[way, step],
+            recv_sem=line_recv.at[way, step],
+            device_id=(there * low + lane, s),
+            device_id_type=MESH,
+        )
+
+    def line_sends(way, step):
+        if way == 0:
+            return (plane < planes - 1) & (plane - step + 1 >= 0)
+        return (plane > 0) & (plane + step - 1 < planes)
+
+    def line_gets(way, step):
+        return plane - step >= 0 if way == 0 else plane + step < planes
+
+    for step in range(1, planes):
+        for way in range(2):
+            @pl.when(line_sends(way, step))
+            def _(way=way, step=step):
+                line_copy(way, step).start()
+        for way in range(2):
+            @pl.when(line_gets(way, step))
+            def _(way=way, step=step):
+                line_copy(way, step).wait_recv()
+
+    def bit_copy(i):
+        part = gathered.at[
+            (slice(None), *(slice(None) if n < i else pl.ds(d, 1) for n, d in enumerate(digits)))
+        ]
+        return pltpu.make_async_remote_copy(
+            src_ref=part,
+            dst_ref=part,
+            send_sem=bit_send.at[i],
+            recv_sem=bit_recv.at[i],
+            device_id=(g ^ (1 << (bits - 1 - i)), s),
+            device_id_type=MESH,
+        )
+
+    for i in range(bits):
+        bit_copy(i).start()
+        bit_copy(i).wait()
 
     def widen(d, carry):
         spread = blocks * heads
         at = pl.ds(pl.multiple_of(d * spread, spread), spread)
         for kv in range(2):
-            wide[kv, at, :] = gathered[d, kv * spread : (kv + 1) * spread].astype(jnp.float32)
+            spot = d // seqs
+            spot = (spot // low, *((spot >> bit) % 2 for bit in reversed(range(bits))), d % seqs)
+            wide[kv, at, :] = gathered[(*spot, pl.ds(kv * spread, spread))].astype(jnp.float32)
         return carry
 
     lax.fori_loop(0, devices, widen, 0)
@@ -221,6 +322,12 @@
     right_bias = jnp.where(has_right, 0.0, -jnp.inf)
 
     def attend(c, carry):
+        if relaying:
+            @pl.when(far & odd & (c < passing))
+            def _():
+                for kv in range(2):
+                    pass_on(kv, c)
+
         for side, there in ((0, has_left), (1, has_right)):
             @pl.when(there)
             def _(side=side):
@@ -274,15 +381,30 @@
 
     lax.fori_loop(0, chunks, attend, 0)
 
-    def finish(c, carry):
-        for side, there in ((0, has_right), (1, has_left)):
-            @pl.when(there)
-            def _(side=side):
-                for kv in range(2):
-                    edge(side, kv, c).wait_send()
-        return carry
-
-    lax.fori_loop(0, chunks, finish, 0)
+    for side in range(2):
+        @pl.when(exists(side))
+        def _(side=side):
+            each(0, chunks, lambda kv, c: edge(side, kv, c).wait_send())
+
+    if relaying:
+        @pl.when(far)
+        def _():
+            each(0, passing, lambda kv, c: forward(kv, c).wait_send())
+
+    for step in range(1, planes):
+        for way in range(2):
+            @pl.when(line_sends(way, step))
+            def _(way=way, step=step):
+                line_copy(way, step).wait_send()
+
+
+def gather_shape(groups):
+    bits = min(groups.bit_length() - 1, PLANE_BITS)
+    return bits, groups >> bits
+
+
+def relays(groups, seqs):
+    return seqs == 2 and groups >= 8
 
 
 def solution(mesh):
@@ -294,9 +416,9 @@
         blocks, heads = rows // BLOCK, width // HEAD_DIM
         devices = groups * seqs
         chunks = heads // CHUNK_HEADS
-        stages = groups.bit_length() - 1
+        bits, planes = gather_shape(groups)
         summaries = devices * blocks * width
-        limit = 2 * (4 * rows + 4 * BLOCK) * width + 12 * summaries + (8 << 20)
+        limit = 2 * (4 * rows + 6 * BLOCK) * width + 12 * summaries + (8 << 20)
         operands = [
             pltpu.with_memory_space_constraint(a, pltpu.HBM)
             for a in (global_pos, layout, queries, keys, values)
@@ -313,17 +435,22 @@
                 pltpu.VMEM((rows, width), jnp.bfloat16),
                 pltpu.VMEM((rows, width), jnp.bfloat16),
                 pltpu.VMEM((2, 2, BLOCK, width), jnp.bfloat16),
-                pltpu.VMEM((devices, 2 * blocks * heads, HEAD_DIM), jnp.bfloat16),
+                pltpu.VMEM((2, BLOCK, width), jnp.bfloat16),
+                pltpu.VMEM((planes, *(2,) * bits, seqs, 2 * blocks * heads, HEAD_DIM), jnp.bfloat16),
                 pltpu.VMEM((2 * blocks * heads, HEAD_DIM), jnp.float32),
                 pltpu.VMEM((2, devices * blocks * heads, HEAD_DIM), jnp.float32),
                 pltpu.VMEM((rows, devices * blocks), jnp.float32),
                 pltpu.SemaphoreType.DMA((5,)),
                 pltpu.SemaphoreType.DMA((2, 2, chunks)),
                 pltpu.SemaphoreType.DMA((2, 2, chunks)),
+                pltpu.SemaphoreType.DMA((2, chunks)),
+                pltpu.SemaphoreType.DMA((2, chunks)),
                 pltpu.SemaphoreType.DMA((seqs,)),
                 pltpu.SemaphoreType.DMA((seqs,)),
-                pltpu.SemaphoreType.DMA((max(stages, 1),)),
-                pltpu.SemaphoreType.DMA((max(stages, 1),)),
+                pltpu.SemaphoreType.DMA((2, planes)),
+                pltpu.SemaphoreType.DMA((2, planes)),
+                pltpu.SemaphoreType.DMA((max(bits, 1),)),
+                pltpu.SemaphoreType.DMA((max(bits, 1),)),
             ],
             compiler_params=pltpu.CompilerParams(
                 collective_id=0, has_side_effects=True, vmem_limit_bytes=limit

time: 101 us -> 97.4 us (0.964)
  the two profiles are of different devices: /device:TPU:0 before, /device:TPU:1 now
where the time goes in v1:
time: 97.4 us; the launch traced here: 97.3 us
  Pallas kernels  96 us (99%)
  local copies, waits for them, and re-layouts  1.32 us (1%)
    pallas_call x1, Pallas kernels, shards(): pl.pallas_call(functools.partial(kernel, groups, seqs), out_shape=pltpu.V...  96 us

profile of v1, /device:TPU:1, one launch (start us, length us, event | category | flops | bytes accessed | tf_op | source)
XLA Modules:
  0.0 97.3 jit_solution(16834805753071487018)
XLA Ops:
  0.0 96.0 %shard_map.55 = bf16[256,4096]{1,0:T(8,128)(2,1)S(1)} custom-call(s32[2]{0:T(128)} %pos_hbm.1, s32[2,32]{1,0:T(2,128)} %layout_hbm.1, bf16[256,4096]{1,0:T(8,128)(2,1)} %q_hbm.1, bf16[256,4096]{1,0:T(8,128)(2,1)} %k_hbm.1, bf16[256,4096]{1,0:T(8,128)(2,1)} %v_hbm.1), custom_call_target="tpu_custom_call" | custom-call | tf_op jit(solution)/shard_map/pallas_call | solution.py:426
  96.0 1.3 %copy.7 = bf16[256,4096]{1,0:T(8,128)(2,1)} copy(bf16[256,4096]{1,0:T(8,128)(2,1)S(1)} %shard_map.55) | data formatting | bytes 4194304

commit v2 on v1

v2 whole, which is shorter than its diff:
```python
import functools
import math

import jax
import jax.numpy as jnp
from jax import lax
from jax.experimental import pallas as pl
from jax.experimental.pallas import tpu as pltpu
from jax.sharding import PartitionSpec as P

HEAD_DIM = 128
BLOCK = 128
STEP_HEADS = 2
UNIT_HEADS = 4
TAPER = (2, 1, 1)
EARLY_UNITS = 1
LEAD_UNITS = 1
PLANE_BITS = 2
POOL_HEADS = 8
MESH = pl.DeviceIdType.MESH


def dot_t(a, b):
    return lax.dot_general(a, b, (((1,), (1,)), ((), ())), preferred_element_type=jnp.float32)


def dot(a, b):
    return jnp.dot(a, b, preferred_element_type=jnp.float32)


def kernel(
    groups, seqs, pos_hbm, layout_hbm, q_hbm, k_hbm, v_hbm, out,
    pos_ref, layout_ref, q, kv_own, halo, relay, gathered, own, wide, bias,
    load_sem, send_sem, recv_sem, relay_recv, relay_send, seq_send, seq_recv,
    line_send, line_recv, bit_send, bit_recv,
):
    rows, width = q.shape
    k, v = kv_own.at[0], kv_own.at[1]
    heads = width // HEAD_DIM
    blocks = rows // BLOCK
    devices = groups * seqs
    total_blocks = devices * blocks
    bits, planes = gather_shape(groups)
    low = 1 << bits
    relaying = relays(groups, seqs)

    g, s = lax.axis_index("grp"), lax.axis_index("seq")
    me = g * seqs + s
    has_left, has_right = me > 0, me < devices - 1
    plane, lane = g // low, g % low

    def coords(position):
        return (position // seqs, position % seqs)

    first = s % 2
    second = 1 - first

    def exists(side):
        return jnp.where(side == 0, has_right, has_left)

    def neighbour(side):
        return jnp.clip(me + 1 - 2 * side, 0, devices - 1)

    pairs = groups // 2
    step_pair = 2 * seqs
    far = (g % 2 == s) if relaying else False
    rank = jnp.where(s == 0, g // 2, pairs - 1 - g // 2)
    odd = rank % 2 == 1
    across = me + (step_pair - 1) * (1 - 2 * s)
    behind, ahead = me + step_pair * (1 - 2 * s), me - step_pair * (1 - 2 * s)
    handed = jnp.where(far, heads * jnp.where(odd, 1, rank) // (pairs * UNIT_HEADS), 0) if relaying else 0
    via = jnp.where(odd, ahead, across)
    passing = heads * jnp.where(odd, pairs - 1 - rank, 1) // (pairs * UNIT_HEADS)
    target = jnp.where(odd, behind, across)
    target_side = jnp.where(odd, first, second)
    apart = (s == 1) & (g < 2) if relaying else False
    lead, lead_relay = apart & (g == 0), apart & (g == 1)
    hand_side = jnp.where(lead, first, second)
    if relaying:
        handed = jnp.where(lead, LEAD_UNITS, handed)
        via = jnp.where(lead, me + seqs, via)
        passing = jnp.where(lead_relay, LEAD_UNITS, passing)
        target = jnp.where(lead_relay, across, target)
    at_once = jnp.logical_not(odd) | lead_relay

    units, taper = edge_units(heads)
    early = min(EARLY_UNITS, units)
    split = early * UNIT_HEADS * HEAD_DIM
    ahead_cols, rest_cols = pl.ds(0, split), pl.ds(split, width - split)
    moves = [(x.at[:, part], y.at[:, part]) for part in (ahead_cols, rest_cols) for x, y in ((k_hbm, k), (v_hbm, v))]
    moves += [(q_hbm, q), (pos_hbm, pos_ref), (layout_hbm, layout_ref)]
    loads = [pltpu.make_async_copy(x, y, load_sem.at[i]) for i, (x, y) in enumerate(moves)]
    for load in loads[:2]:
        load.start()
    barrier = pltpu.get_barrier_semaphore()

    peers = [(exists(side), neighbour(side)) for side in range(2)]
    peers += [(True, g * seqs + lax.rem(s + o, seqs)) for o in range(1, seqs)]
    peers += [(True, (g ^ (1 << bit)) * seqs + s) for bit in range(bits)]
    if planes > 1:
        peers += [
            (plane > 0, jnp.maximum(me - low * seqs, 0)),
            (plane < planes - 1, jnp.minimum(me + low * seqs, devices - 1)),
        ]
    if relaying:
        peers += [(far, across), (far & (rank > 0), ahead), (far & (rank < pairs - 1), behind)]
    expected = 0
    for there, peer in peers:
        if there is True:
            pl.semaphore_signal(barrier, inc=1, device_id=coords(peer), device_id_type=MESH)
            expected = expected + 1
        else:
            @pl.when(there)
            def _(peer=peer):
                pl.semaphore_signal(barrier, inc=1, device_id=coords(peer), device_id_type=MESH)
            expected = expected + there.astype(jnp.int32)
    for load in loads[2:]:
        load.start()
    pl.semaphore_wait(barrier, expected)

    def columns(h):
        return pl.ds(pl.multiple_of(h * HEAD_DIM, HEAD_DIM), HEAD_DIM)

    def span(u):
        if isinstance(u, int) and u >= units:
            lo, n = taper[u - units]
            return pl.ds(lo * HEAD_DIM, n * HEAD_DIM)
        return pl.ds(pl.multiple_of(u * UNIT_HEADS * HEAD_DIM, UNIT_HEADS * HEAD_DIM), UNIT_HEADS * HEAD_DIM)

    def edge(side, u):
        start = pl.multiple_of((rows - BLOCK) * (1 - side), BLOCK)
        return pltpu.make_async_remote_copy(
            src_ref=kv_own.at[:, pl.ds(start, BLOCK), span(u)],
            dst_ref=halo.at[side, :, :, span(u)],
            send_sem=send_sem.at[side, u],
            recv_sem=recv_sem.at[side, u],
            device_id=coords(neighbour(side)),
            device_id_type=MESH,
        )

    def hand(u):
        start = pl.multiple_of((rows - BLOCK) * (1 - hand_side), BLOCK)
        return pltpu.make_async_remote_copy(
            src_ref=kv_own.at[:, pl.ds(start, BLOCK), span(u)],
            dst_ref=relay.at[:, :, span(u)],
            send_sem=send_sem.at[hand_side, u],
            recv_sem=relay_recv.at[u],
            device_id=coords(jnp.clip(via, 0, devices - 1)),
            device_id_type=MESH,
        )

    def forward(u):
        return pltpu.make_async_remote_copy(
            src_ref=relay.at[:, :, span(u)],
            dst_ref=halo.at[target_side, :, :, span(u)],
            send_sem=relay_send.at[u],
            recv_sem=recv_sem.at[target_side, u],
            device_id=coords(jnp.clip(target, 0, devices - 1)),
            device_id_type=MESH,
        )

    def pass_on(u):
        hand(u).wait_recv()
        forward(u).start()

    def each(lo, hi, act):
        def body(u, carry):
            act(u)
            return carry

        lax.fori_loop(lo, hi, body, 0)

    def every(lo, act):
        each(lo, units, act)
        for i in range(len(taper)):
            act(units + i)

    def send(sides):
        def act(u):
            for side in sides:
                if not relaying or (isinstance(u, int) and u >= units):
                    edge(side, u).start()
                    continue
                stop = (u < handed) & (side == hand_side)

                @pl.when(stop)
                def _():
                    hand(u).start()

                @pl.when(jnp.logical_not(stop))
                def _(side=side):
                    edge(side, u).start()

        return act

    both = exists(first) & exists(second) & jnp.logical_not(apart)

    loads[0].wait()
    loads[1].wait()

    @pl.when(both)
    def _():
        each(0, early, send((first, second)))

    @pl.when(exists(first) & jnp.logical_not(both))
    def _():
        each(0, early, send((first,)))

    loads[2].wait()
    loads[3].wait()
    picks = (
        lax.broadcasted_iota(jnp.int32, (16, rows), 1) // BLOCK
        == lax.broadcasted_iota(jnp.int32, (16, rows), 0)
    ).astype(jnp.bfloat16)

    def pool(step, carry):
        for i in range(POOL_HEADS):
            h = step * POOL_HEADS + i
            cols = columns(h)
            for kv, src in enumerate((k, v)):
                mean = dot(picks, src[:, cols])[:8] * (1.0 / BLOCK)
                spread = jnp.mean(mean * mean, axis=-1, keepdims=True)
                scaled = mean / jnp.sqrt(spread + 1e-06)
                for b in range(blocks):
                    own[pl.ds((kv * blocks + b) * heads + h, 1), :] = scaled[b : b + 1]
        return carry

    lax.fori_loop(0, heads // POOL_HEADS, pool, 0)
    digits = [(lane >> bit) % 2 for bit in reversed(range(bits))]
    gathered[(plane, *digits, s)] = own[...].astype(jnp.bfloat16)

    def seq_copy(o):
        mine = gathered.at[(pl.ds(plane, 1), *(pl.ds(d, 1) for d in digits), pl.ds(s, 1))]
        return pltpu.make_async_remote_copy(
            src_ref=mine,
            dst_ref=mine,
            send_sem=seq_send.at[o],
            recv_sem=seq_recv.at[o],
            device_id=(g, lax.rem(s + o, seqs)),
            device_id_type=MESH,
        )

    for o in range(1, seqs):
        seq_copy(o).start()

    if relaying:
        @pl.when(far & at_once)
        def _():
            each(0, passing, pass_on)

    @pl.when(both)
    def _():
        every(early, send((first, second)))

    @pl.when(exists(first) & jnp.logical_not(both))
    def _():
        every(early, send((first,)))

    @pl.when(exists(second) & apart)
    def _():
        every(0, send((second,)))

    loads[5].wait()
    loads[6].wait()
    ids = lax.broadcasted_iota(jnp.int32, (BLOCK, total_blocks), 1)
    spots = lax.broadcasted_iota(jnp.int32, (BLOCK, total_blocks), 0)
    for b in range(blocks):
        seen = spots == pos_ref[b]
        for link in range(layout_ref.shape[1]):
            seen = seen | (ids == layout_ref[b, link])
        bias[b * BLOCK : (b + 1) * BLOCK, :] = jnp.where(seen, 0.0, -jnp.inf)

    @pl.when(jnp.logical_not(has_left))
    def _():
        halo[0] = jnp.zeros(halo.shape[1:], halo.dtype)

    @pl.when(jnp.logical_not(has_right))
    def _():
        halo[1] = jnp.zeros(halo.shape[1:], halo.dtype)

    for o in range(1, seqs):
        seq_copy(o).wait()

    def line_copy(way, step):
        there = jnp.clip(plane + 1 - 2 * way, 0, planes - 1)
        part = jnp.clip(plane + (step - 1) * (2 * way - 1), 0, planes - 1)
        part = gathered.at[(pl.ds(part, 1), *(pl.ds(d, 1) for d in digits))]
        return pltpu.make_async_remote_copy(
            src_ref=part,
            dst_ref=part,
            send_sem=line_send.at[way, step],
            recv_sem=line_recv.at[way, step],
            device_id=(there * low + lane, s),
            device_id_type=MESH,
        )

    def line_sends(way, step):
        if way == 0:
            return (plane < planes - 1) & (plane - step + 1 >= 0)
        return (plane > 0) & (plane + step - 1 < planes)

    def line_gets(way, step):
        return plane - step >= 0 if way == 0 else plane + step < planes

    for step in range(1, planes):
        for way in range(2):
            @pl.when(line_sends(way, step))
            def _(way=way, step=step):
                line_copy(way, step).start()
        for way in range(2):
            @pl.when(line_gets(way, step))
            def _(way=way, step=step):
                line_copy(way, step).wait_recv()

    def bit_copy(i):
        part = gathered.at[
            (slice(None), *(slice(None) if n < i else pl.ds(d, 1) for n, d in enumerate(digits)))
        ]
        return pltpu.make_async_remote_copy(
            src_ref=part,
            dst_ref=part,
            send_sem=bit_send.at[i],
            recv_sem=bit_recv.at[i],
            device_id=(g ^ (1 << (bits - 1 - i)), s),
            device_id_type=MESH,
        )

    for i in range(bits):
        bit_copy(i).start()
        bit_copy(i).wait()

    def widen(d, carry):
        spread = blocks * heads
        at = pl.ds(pl.multiple_of(d * spread, spread), spread)
        for kv in range(2):
            spot = d // seqs
            spot = (spot // low, *((spot >> bit) % 2 for bit in reversed(range(bits))), d % seqs)
            wide[kv, at, :] = gathered[(*spot, pl.ds(kv * spread, spread))].astype(jnp.float32)
        return carry

    lax.fori_loop(0, devices, widen, 0)
    loads[4].wait()

    factor = math.log2(math.e) / math.sqrt(HEAD_DIM)
    left_bias = jnp.where(has_left, 0.0, -jnp.inf)
    right_bias = jnp.where(has_right, 0.0, -jnp.inf)

    def attend_head(h, ready):
        cols = columns(h)
        rows_of = pl.ds(h, total_blocks, stride=heads)
        qh, kh, vh = q[:, cols], k[:, cols], v[:, cols]
        sk = wide[0, rows_of, :].astype(jnp.bfloat16)
        sv = wide[1, rows_of, :].astype(jnp.bfloat16)
        s_own = dot_t(qh, kh)
        if blocks > 2:
            gap = (
                lax.broadcasted_iota(jnp.int32, (rows, rows), 0) // BLOCK
                - lax.broadcasted_iota(jnp.int32, (rows, rows), 1) // BLOCK
            )
            s_own = jnp.where(jnp.abs(gap) <= 1, s_own, -jnp.inf)
        s_sum = dot_t(qh, sk) + bias[...]
        ready()
        s_left = dot_t(qh[:BLOCK], halo[0, 0, :, cols]) + left_bias
        s_right = dot_t(qh[rows - BLOCK :], halo[1, 0, :, cols]) + right_bias
        middle = [jnp.full((rows - 2 * BLOCK, BLOCK), -jnp.inf)] if blocks > 2 else []
        s_halo = jnp.concatenate([s_left, *middle, s_right], axis=0)
        peak = jnp.maximum(
            jnp.max(s_sum, axis=-1, keepdims=True),
            jnp.maximum(
                jnp.max(s_own, axis=-1, keepdims=True),
                jnp.max(s_halo, axis=-1, keepdims=True),
            ),
        )
        w_own = jnp.exp2((s_own - peak) * factor)
        w_halo = jnp.exp2((s_halo - peak) * factor)
        w_sum = jnp.exp2((s_sum - peak) * factor)
        total = (
            jnp.sum(w_own, axis=-1, keepdims=True)
            + jnp.sum(w_halo, axis=-1, keepdims=True)
            + jnp.sum(w_sum, axis=-1, keepdims=True)
        )
        r_halo = w_halo.astype(jnp.bfloat16)
        acc = dot(w_own.astype(jnp.bfloat16), vh) + dot(w_sum.astype(jnp.bfloat16), sv)
        vl, vr = halo[0, 1, :, cols], halo[1, 1, :, cols]
        middle = [jnp.zeros((rows - 2 * BLOCK, HEAD_DIM), jnp.float32)] if blocks > 2 else []
        acc = acc + jnp.concatenate(
            [dot(r_halo[:BLOCK], vl), *middle, dot(r_halo[rows - BLOCK :], vr)], axis=0
        )
        out[:, cols] = (acc / total).astype(jnp.bfloat16)

    def arrived(u):
        for side, there in ((0, has_left), (1, has_right)):
            @pl.when(there)
            def _(side=side):
                edge(side, u).wait_recv()

    steps = UNIT_HEADS // STEP_HEADS

    def attend(step, carry):
        u = step // steps

        @pl.when(step % steps == 0)
        def _():
            if relaying:
                @pl.when(far & jnp.logical_not(at_once) & (u < passing))
                def _():
                    pass_on(u)

            arrived(u)

        for i in range(STEP_HEADS):
            attend_head(step * STEP_HEADS + i, lambda: None)
        return carry

    lax.fori_loop(0, units * steps, attend, 0)

    def sent(lo, hi):
        for side in range(2):
            @pl.when(exists(side))
            def _(side=side):
                each(lo, hi, lambda u: edge(side, u).wait_send())

    for i, (lo, n) in enumerate(taper):
        if n > 1:
            arrived(units + i)
            for h in range(lo, lo + n):
                attend_head(h, lambda: None)
            continue
        if i + 1 == len(taper):
            sent(0, units)
            if relaying:
                @pl.when(far)
                def _():
                    each(0, passing, lambda u: forward(u).wait_send())

            for step in range(1, planes):
                for way in range(2):
                    @pl.when(line_sends(way, step))
                    def _(way=way, step=step):
                        line_copy(way, step).wait_send()

        attend_head(lo, lambda i=i: arrived(units + i))

    for side in range(2):
        @pl.when(exists(side))
        def _(side=side):
            for i in range(len(taper)):
                edge(side, units + i).wait_send()


def edge_units(heads):
    units = (heads - sum(TAPER)) // UNIT_HEADS
    lo, taper = units * UNIT_HEADS, []
    for n in (heads - lo - sum(TAPER), *TAPER):
        if n:
            taper.append((lo, n))
            lo += n
    return units, taper


def gather_shape(groups):
    bits = min(groups.bit_length() - 1, PLANE_BITS)
    return bits, groups >> bits


def relays(groups, seqs):
    return seqs == 2 and groups >= 8


def solution(mesh):
    groups, seqs = mesh.shape["grp"], mesh.shape["seq"]
    assert groups & (groups - 1) == 0

    def shards(queries, keys, values, global_pos, layout):
        rows, width = queries.shape
        blocks, heads = rows // BLOCK, width // HEAD_DIM
        devices = groups * seqs
        units, taper = edge_units(heads)
        units += len(taper)
        bits, planes = gather_shape(groups)
        summaries = devices * blocks * width
        limit = 2 * (4 * rows + 6 * BLOCK) * width + 12 * summaries + (8 << 20)
        operands = [
            pltpu.with_memory_space_constraint(a, pltpu.HBM)
            for a in (global_pos, layout, queries, keys, values)
        ]
        return pl.pallas_call(
            functools.partial(kernel, groups, seqs),
            out_shape=pltpu.VMEM((rows, width), jnp.bfloat16),
            in_specs=[pl.BlockSpec(memory_space=pltpu.HBM)] * 5,
            out_specs=pl.BlockSpec(memory_space=pltpu.VMEM),
            scratch_shapes=[
                pltpu.SMEM(global_pos.shape, jnp.int32),
                pltpu.SMEM(layout.shape, jnp.int32),
                pltpu.VMEM((rows, width), jnp.bfloat16),
                pltpu.VMEM((2, rows, width), jnp.bfloat16),
                pltpu.VMEM((2, 2, BLOCK, width), jnp.bfloat16),
                pltpu.VMEM((2, BLOCK, width), jnp.bfloat16),
                pltpu.VMEM((planes, *(2,) * bits, seqs, 2 * blocks * heads, HEAD_DIM), jnp.bfloat16),
                pltpu.VMEM((2 * blocks * heads, HEAD_DIM), jnp.float32),
                pltpu.VMEM((2, devices * blocks * heads, HEAD_DIM), jnp.float32),
                pltpu.VMEM((rows, devices * blocks), jnp.float32),
                pltpu.SemaphoreType.DMA((7,)),
                pltpu.SemaphoreType.DMA((2, units)),
                pltpu.SemaphoreType.DMA((2, units)),
                pltpu.SemaphoreType.DMA((units,)),
                pltpu.SemaphoreType.DMA((units,)),
                pltpu.SemaphoreType.DMA((seqs,)),
                pltpu.SemaphoreType.DMA((seqs,)),
                pltpu.SemaphoreType.DMA((2, planes)),
                pltpu.SemaphoreType.DMA((2, planes)),
                pltpu.SemaphoreType.DMA((max(bits, 1),)),
                pltpu.SemaphoreType.DMA((max(bits, 1),)),
            ],
            compiler_params=pltpu.CompilerParams(
                collective_id=0, has_side_effects=True, vmem_limit_bytes=limit
            ),
        )(*operands)

    both = ("grp", "seq")
    in_specs = (P(both, None), P(both, None), P(both, None), P(both), P(both, None))
    return jax.shard_map(
        shards, mesh=mesh, in_specs=in_specs, out_specs=P(both, None), check_vma=False
    )
```

time: 97.4 us -> 95.3 us (0.978)
  Pallas kernels: 96 us -> 93.8 us
    pallas_call x1, Pallas kernels: 96 us -> 93.8 us  [shards(): pl.pallas_call(functools.partial(kernel, groups, seqs), out_shape=pltpu.V...]
where the time goes in v2:
time: 95.3 us; the launch traced here: 95.1 us
  Pallas kernels  93.8 us (98%)
  local copies, waits for them, and re-layouts  1.32 us (1%)
    pallas_call x1, Pallas kernels, shards(): pl.pallas_call(functools.partial(kernel, groups, seqs), out_shape=pltpu.V...  93.8 us

profile of v2, /device:TPU:1, one launch (start us, length us, event | category | flops | bytes accessed | tf_op | source)
XLA Modules:
  0.0 95.1 jit_solution(4019939701893774038)
XLA Ops:
  0.0 93.8 %shard_map.55 = bf16[256,4096]{1,0:T(8,128)(2,1)S(1)} custom-call(s32[2]{0:T(128)} %pos_hbm.1, s32[2,32]{1,0:T(2,128)} %layout_hbm.1, bf16[256,4096]{1,0:T(8,128)(2,1)} %q_hbm.1, bf16[256,4096]{1,0:T(8,128)(2,1)} %k_hbm.1, bf16[256,4096]{1,0:T(8,128)(2,1)} %v_hbm.1), custom_call_target="tpu_custom_call" | custom-call | tf_op jit(solution)/shard_map/pallas_call | solution.py:487
  93.8 1.3 %copy.7 = bf16[256,4096]{1,0:T(8,128)(2,1)} copy(bf16[256,4096]{1,0:T(8,128)(2,1)S(1)} %shard_map.55) | data formatting | bytes 4194304

commit v3 on v2

--- a/solution.py
+++ b/solution.py
@@ -15,6 +15,8 @@
 TAPER = (2, 1, 1)
 EARLY_UNITS = 1
 LEAD_UNITS = 1
+LEAD_TAPER = 1
+SWAP = True
 PLANE_BITS = 2
 POOL_HEADS = 8
 MESH = pl.DeviceIdType.MESH
@@ -90,12 +92,13 @@
     moves = [(x.at[:, part], y.at[:, part]) for part in (ahead_cols, rest_cols) for x, y in ((k_hbm, k), (v_hbm, v))]
     moves += [(q_hbm, q), (pos_hbm, pos_ref), (layout_hbm, layout_ref)]
     loads = [pltpu.make_async_copy(x, y, load_sem.at[i]) for i, (x, y) in enumerate(moves)]
-    for load in loads[:2]:
-        load.start()
     barrier = pltpu.get_barrier_semaphore()
 
-    peers = [(exists(side), neighbour(side)) for side in range(2)]
-    peers += [(True, g * seqs + lax.rem(s + o, seqs)) for o in range(1, seqs)]
+    peers = [(True, g * seqs + lax.rem(s + o, seqs)) for o in range(1, seqs)]
+    if seqs == 2:
+        peers += [(exists(second), neighbour(second))]
+    else:
+        peers += [(exists(side), neighbour(side)) for side in range(2)]
     peers += [(True, (g ^ (1 << bit)) * seqs + s) for bit in range(bits)]
     if planes > 1:
         peers += [
@@ -114,7 +117,7 @@
             def _(peer=peer):
                 pl.semaphore_signal(barrier, inc=1, device_id=coords(peer), device_id_type=MESH)
             expected = expected + there.astype(jnp.int32)
-    for load in loads[2:]:
+    for load in loads:
         load.start()
     pl.semaphore_wait(barrier, expected)
 
@@ -178,10 +181,10 @@
     def send(sides):
         def act(u):
             for side in sides:
-                if not relaying or (isinstance(u, int) and u >= units):
+                if not relaying or (isinstance(u, int) and u >= units and u != units + LEAD_TAPER):
                     edge(side, u).start()
                     continue
-                stop = (u < handed) & (side == hand_side)
+                stop = (lead if isinstance(u, int) and u >= units else u < handed) & (side == hand_side)
 
                 @pl.when(stop)
                 def _():
@@ -193,6 +196,7 @@
 
         return act
 
+    ahead_side = jnp.where((s == 1) & (g % 2 == 0), second, first) if SWAP else first
     both = exists(first) & exists(second) & jnp.logical_not(apart)
 
     loads[0].wait()
@@ -200,7 +204,7 @@
 
     @pl.when(both)
     def _():
-        each(0, early, send((first, second)))
+        each(0, early, send((ahead_side, 1 - ahead_side)))
 
     @pl.when(exists(first) & jnp.logical_not(both))
     def _():
@@ -248,9 +252,13 @@
         def _():
             each(0, passing, pass_on)
 
+        @pl.when(lead_relay)
+        def _():
+            pass_on(units + LEAD_TAPER)
+
     @pl.when(both)
     def _():
-        every(early, send((first, second)))
+        every(early, send((ahead_side, 1 - ahead_side)))
 
     @pl.when(exists(first) & jnp.logical_not(both))
     def _():
@@ -421,11 +429,6 @@
                 each(lo, hi, lambda u: edge(side, u).wait_send())
 
     for i, (lo, n) in enumerate(taper):
-        if n > 1:
-            arrived(units + i)
-            for h in range(lo, lo + n):
-                attend_head(h, lambda: None)
-            continue
         if i + 1 == len(taper):
             sent(0, units)
             if relaying:
@@ -433,13 +436,18 @@
                 def _():
                     each(0, passing, lambda u: forward(u).wait_send())
 
+                @pl.when(lead_relay)
+                def _():
+                    forward(units + LEAD_TAPER).wait_send()
+
             for step in range(1, planes):
                 for way in range(2):
                     @pl.when(line_sends(way, step))
                     def _(way=way, step=step):
                         line_copy(way, step).wait_send()
 
-        attend_head(lo, lambda i=i: arrived(units + i))
+        for h in range(lo, lo + n):
+            attend_head(h, (lambda i=i: arrived(units + i)) if h == lo else lambda: None)
 
     for side in range(2):
         @pl.when(exists(side))

time: 95.3 us -> 94.6 us (level)
    pallas_call x1, Pallas kernels: 93.8 us -> 92.9 us  [shards(): pl.pallas_call(functools.partial(kernel, groups, seqs), out_shape=pltpu.V...]
where the time goes in v3:
time: 94.6 us; the launch traced here: 94.2 us
  Pallas kernels  92.9 us (98%)
  local copies, waits for them, and re-layouts  1.32 us (1%)
    pallas_call x1, Pallas kernels, shards(): pl.pallas_call(functools.partial(kernel, groups, seqs), out_shape=pltpu.V...  92.9 us

profile of v3, /device:TPU:1, one launch (start us, length us, event | category | flops | bytes accessed | tf_op | source)
XLA Modules:
  0.0 94.2 jit_solution(6986704051296694215)
XLA Ops:
  0.0 92.9 %shard_map.55 = bf16[256,4096]{1,0:T(8,128)(2,1)S(1)} custom-call(s32[2]{0:T(128)} %pos_hbm.1, s32[2,32]{1,0:T(2,128)} %layout_hbm.1, bf16[256,4096]{1,0:T(8,128)(2,1)} %q_hbm.1, bf16[256,4096]{1,0:T(8,128)(2,1)} %k_hbm.1, bf16[256,4096]{1,0:T(8,128)(2,1)} %v_hbm.1), custom_call_target="tpu_custom_call" | custom-call | tf_op jit(solution)/shard_map/pallas_call | solution.py:495
  92.9 1.3 %copy.7 = bf16[256,4096]{1,0:T(8,128)(2,1)} copy(bf16[256,4096]{1,0:T(8,128)(2,1)S(1)} %shard_map.55) | data formatting | bytes 4194304

commit v4 on v3

--- a/solution.py
+++ b/solution.py
@@ -92,6 +92,8 @@
     moves = [(x.at[:, part], y.at[:, part]) for part in (ahead_cols, rest_cols) for x, y in ((k_hbm, k), (v_hbm, v))]
     moves += [(q_hbm, q), (pos_hbm, pos_ref), (layout_hbm, layout_ref)]
     loads = [pltpu.make_async_copy(x, y, load_sem.at[i]) for i, (x, y) in enumerate(moves)]
+    for load in loads[:4]:
+        load.start()
     barrier = pltpu.get_barrier_semaphore()
 
     peers = [(True, g * seqs + lax.rem(s + o, seqs)) for o in range(1, seqs)]
@@ -117,7 +119,7 @@
             def _(peer=peer):
                 pl.semaphore_signal(barrier, inc=1, device_id=coords(peer), device_id_type=MESH)
             expected = expected + there.astype(jnp.int32)
-    for load in loads:
+    for load in loads[4:]:
         load.start()
     pl.semaphore_wait(barrier, expected)
 

time: 94.6 us -> 94.7 us (level)
  no operation moved by 1% of the time
where the time goes in v4:
time: 94.7 us; the launch traced here: 94.2 us
  Pallas kernels  92.9 us (98%)
  local copies, waits for them, and re-layouts  1.32 us (1%)
    pallas_call x1, Pallas kernels, shards(): pl.pallas_call(functools.partial(kernel, groups, seqs), out_shape=pltpu.V...  92.9 us

profile of v4, /device:TPU:1, one launch (start us, length us, event | category | flops | bytes accessed | tf_op | source)
XLA Modules:
  0.0 94.2 jit_solution(9777941135796625387)
XLA Ops:
  0.0 92.9 %shard_map.55 = bf16[256,4096]{1,0:T(8,128)(2,1)S(1)} custom-call(s32[2]{0:T(128)} %pos_hbm.1, s32[2,32]{1,0:T(2,128)} %layout_hbm.1, bf16[256,4096]{1,0:T(8,128)(2,1)} %q_hbm.1, bf16[256,4096]{1,0:T(8,128)(2,1)} %k_hbm.1, bf16[256,4096]{1,0:T(8,128)(2,1)} %v_hbm.1), custom_call_target="tpu_custom_call" | custom-call | tf_op jit(solution)/shard_map/pallas_call | solution.py:497
  92.9 1.3 %copy.7 = bf16[256,4096]{1,0:T(8,128)(2,1)} copy(bf16[256,4096]{1,0:T(8,128)(2,1)S(1)} %shard_map.55) | data formatting | bytes 4194304
